TPU v7x, 1024 devices: a whole 4x4x32 slice. The times are simulated.
1024 devices in a mesh: gx: 64 (over z_lo, x, core), gy: 16 (over y, z_hi).
Axes of the slice: x: 4, y: 4, z: 32 (z_hi: 4, z_lo: 8; z = z_hi * 8 + z_lo), core: 2. Of those that a mesh axis runs over, the one named last changes fastest.
Arguments:
- prefix_tokens: bfloat16 [49152, 8192], P('gx'), may hold values from -6 to 6
- key_value_weight: bfloat16 [8192, 2048], P('gx', 'gy'), may hold values from -0.0625 to 0.0625
- prefix_lengths: int32 [384], P('gx'), may hold values from 1 to 128, as said below
- start_offsets: int32 [384], P('gx'), may hold values from 0 to 8064
- queries: bfloat16 [32, 8192], P('gy'), may hold values from -5 to 5
- key_value_cache: bfloat16 [2, 32, 8192, 1024], P(None, 'gy', 'gx'), may hold values from -5 to 5
- cache_lengths: int32 [32], P('gy'), may hold values from 1024 to 8192, as said below
- out_weight: bfloat16 [8192, 8192], P('gy', 'gx'), may hold values from -0.5 to 0.5
Outputs:
- prefix_kv: bfloat16 [49152, 2048], P('gx', 'gy')
- decode_out: bfloat16 [32, 8192], P('gy', 'gx')
Inputs may be any that keep to these rules, and one draw needn't show every extreme that they name: `prefix_lengths`: live tokens stand at the front of a prefix's slots; in every draw some prefix uses all 128 slots. `cache_lengths`: live positions stand at the front of a trajectory's cache; in every draw some trajectory uses all 8192 positions.
All inputs are finite; a program needn't handle non-finite values.
Results may differ from a plain program's by a relative error of at most 0.0051.
Values may be sent and summed in bfloat16 or wider, within the bound.
A program may use at most 64 MiB of HBM per device.

v0:
```python
import jax
import jax.numpy as jnp
from jax import lax
from jax.sharding import Mesh
from jax.sharding import PartitionSpec as P

QUERY_HEADS = 64
KEY_VALUE_HEADS = 8
HEAD_SIZE = 128
SLOT = 128
GX = ("gx_0", "gx_1", "gx_2")


rope_base = 500000.0
masked_score = -1e30


def all_in_one(shard, axis):
    leaves = jax.tree.leaves(shard)
    order = sorted(range(len(leaves)), key=lambda k: -leaves[k].size)
    width = (1, *leaves[order[0]].shape)[-1]
    lines = [
        jnp.pad(leaves[k].reshape(-1), (0, -leaves[k].size % width)).reshape(-1, width)
        for k in order
    ]
    both, at, found = (lax.all_gather(jnp.concatenate(lines), axis), 0, {})
    for k, line in zip(order, lines):
        slab = both[:, at : at + len(line)].reshape(len(both), -1)
        found[k] = slab[:, : leaves[k].size].reshape(-1, *leaves[k].shape)
        at += len(line)
    numbers = iter(range(len(leaves)))
    return jax.tree.map(lambda _: found[next(numbers)], shard)


def joined_all(shard, axes, combine):
    for axis in axes:
        pieces = all_in_one(shard, axis)
        shard = jax.tree.map(lambda part: part[0], pieces)
        for k in range(1, lax.axis_size(axis)):
            shard = combine(shard, jax.tree.map(lambda part: part[k], pieces))
    return shard


def cut_along(shard, dim, devices):
    dims = shard.shape
    tiles = shard.reshape(*dims[:dim], devices, dims[dim] // devices, *dims[dim + 1 :])
    return jnp.moveaxis(tiles, dim, 0)


def sum_at_owner(shard, axis, dim):
    devices = lax.axis_size(axis)
    tiles = lax.all_to_all(cut_along(shard, dim, devices), axis, 0, 0, tiled=True)
    return jnp.sum(tiles, axis=0)


def rotate_and_mask(projected, first_column, prefix_lengths, start_offsets):
    tok_rows, columns = projected.shape
    slot_index = jnp.arange(SLOT, dtype=jnp.int32)
    positions = (start_offsets[:, None] + slot_index[None, :]).reshape(tok_rows)
    live_rows = (slot_index[None, :] < prefix_lengths[:, None]).reshape(tok_rows)
    half_width = HEAD_SIZE // 2
    freq_index = jnp.arange(half_width, dtype=jnp.float32)
    inverse = rope_base ** (-2.0 * freq_index / HEAD_SIZE)
    angles = positions.astype(jnp.float32)[:, None] * inverse[None, :]
    cosine = jnp.cos(angles)[:, None, :]
    sine = jnp.sin(angles)[:, None, :]
    head_list = projected.reshape(tok_rows, columns // HEAD_SIZE, HEAD_SIZE)
    first_half = head_list[:, :, :half_width]
    second_half = head_list[:, :, half_width:]
    rotary_applied = jnp.concatenate(
        [first_half * cosine - second_half * sine, second_half * cosine + first_half * sine], axis=2
    )
    head_position = first_column // HEAD_SIZE + jnp.arange(columns // HEAD_SIZE, dtype=jnp.int32)
    key_tagged = jnp.where(
        (head_position < KEY_VALUE_HEADS)[None, :, None], rotary_applied, head_list
    )
    kept = jnp.where(live_rows[:, None, None], key_tagged, 0.0)
    return kept.reshape(tok_rows, columns).astype(jnp.bfloat16)


def merge_parts(earlier, later):
    highest = jnp.maximum(earlier[0], later[0])
    early_factor = jnp.exp(earlier[0] - highest)
    late_factor = jnp.exp(later[0] - highest)
    summed = earlier[1] * early_factor + later[1] * late_factor
    weighted = earlier[2] * early_factor[..., None] + later[2] * late_factor[..., None]
    return (highest, summed, weighted)


def shards(
    prefix_tokens,
    key_value_weight,
    prefix_lengths,
    start_offsets,
    queries,
    key_value_cache,
    cache_lengths,
    out_weight,
):
    columns = key_value_weight.shape[1]
    selected = prefix_tokens
    projected = jnp.dot(
        selected,
        lax.all_gather(key_value_weight, GX, axis=0, tiled=True),
        preferred_element_type=jnp.float32,
    )
    prefix_kv = rotate_and_mask(
        projected, lax.axis_index("gy") * columns, prefix_lengths, start_offsets
    )
    trajectory_per_shard = queries.shape[0]
    cache_per_shard = key_value_cache.shape[2]
    query_group = QUERY_HEADS // KEY_VALUE_HEADS
    query_head_rows = queries.reshape(trajectory_per_shard, KEY_VALUE_HEADS, query_group, HEAD_SIZE)
    key_rows = key_value_cache[0].reshape(
        trajectory_per_shard, cache_per_shard, KEY_VALUE_HEADS, HEAD_SIZE
    )
    value_rows = key_value_cache[1].reshape(
        trajectory_per_shard, cache_per_shard, KEY_VALUE_HEADS, HEAD_SIZE
    )
    scores = jnp.einsum(
        "bhgd,bphd->bhgp", query_head_rows, key_rows, preferred_element_type=jnp.float32
    ) * HEAD_SIZE ** (-0.5)
    position = lax.axis_index(GX) * cache_per_shard + jnp.arange(cache_per_shard, dtype=jnp.int32)
    valid = (position[None, :] < cache_lengths[:, None])[:, None, None, :]
    peak = jnp.max(jnp.where(valid, scores, masked_score), axis=3)
    weights = jnp.where(valid, jnp.exp(scores - peak[..., None]), 0.0)
    block_total = jnp.sum(weights, axis=3)
    numerator = jnp.einsum(
        "bhgp,bphd->bhgd",
        weights.astype(jnp.bfloat16),
        value_rows,
        preferred_element_type=jnp.float32,
    )
    peak, block_total, numerator = joined_all((peak, block_total, numerator), GX, merge_parts)
    attention = (
        (numerator / block_total[..., None])
        .reshape(trajectory_per_shard, QUERY_HEADS * HEAD_SIZE)
        .astype(jnp.bfloat16)
    )
    spread = lax.all_to_all(attention, "gy", split_axis=1, concat_axis=0, tiled=True)
    selected = spread
    mixed = sum_at_owner(jnp.dot(selected, out_weight, preferred_element_type=jnp.float32), "gy", 0)
    return (prefix_kv, mixed.astype(jnp.bfloat16))


def solution(mesh):
    finer = Mesh(mesh.devices.reshape(8, 4, 2, mesh.shape["gy"]), ("gx_0", "gx_1", "gx_2", "gy"))
    return jax.shard_map(
        shards,
        mesh=finer,
        in_specs=(
            P(GX, None),
            P(GX, "gy"),
            P(GX),
            P(GX),
            P("gy", None),
            P(None, "gy", GX, None),
            P("gy"),
            P("gy", GX),
        ),
        out_specs=(P(GX, "gy"), P("gy", GX)),
        check_vma=False,
    )
```

profile of v0, /device:TPU:2, one launch (start us, length us, event | category | flops | bytes accessed | tf_op | source)
XLA Modules:
  0.0 180.2 jit_solution(8867225095857639104)
XLA Ops:
  7.2 0.0 copy-start
  7.2 0.0 all-gather.8.cloned.1.call-start
  7.2 0.7 all-gather.8.cloned.1.call-update
  7.9 1.3 fusion.115
  9.2 0.3 copy.35
  9.5 0.7 broadcast_compare_fusion
  10.2 1.1 select_reduce_fusion
  11.3 0.1 reshape.1294
  11.4 0.2 fusion.42
  11.6 0.1 reshape.1295
  11.7 0.3 copy.36
  11.9 0.4 fusion.44
  12.4 50.6 %all-gather.3 = f32[8,130,128]{2,1,0:T(8,128)S(1)} all-gather(f32[1,130,128]{2,1,0:T(8,128)S(1)} %maximum_bitcast_fusion), channel_id=2, replica_groups=mesh['gx_0'=8,'gx_1'=4,'gx_2'=2,'gy'=16] {'gx_0'}, dimensions={0}, use_global_device_ids=true | all-gather | bytes 599040 | tf_op jit(solution)/shard_map/all_gather | solution.py:26
  63.1 0.3 fusion.22
  63.4 19.9 %all-gather.4 = f32[4,130,128]{2,1,0:T(8,128)S(1)} all-gather(f32[1,130,128]{2,1,0:T(8,128)S(1)} %maximum_bitcast_fusion.1), channel_id=3, replica_groups=mesh['gx_0'=8,'gx_1'=4,'gx_2'=2,'gy'=16] {'gx_1'}, dimensions={0}, use_global_device_ids=true | all-gather | bytes 332800 | tf_op jit(solution)/shard_map/all_gather | solution.py:26
  83.3 0.2 fusion.13
  83.5 1.9 %all-gather.5 = f32[2,130,128]{2,1,0:T(8,128)S(1)} all-gather(f32[1,130,128]{2,1,0:T(8,128)S(1)} %maximum_bitcast_fusion.2), channel_id=4, replica_groups=mesh['gx_0'=8,'gx_1'=4,'gx_2'=2,'gy'=16] {'gx_2'}, dimensions={0}, use_global_device_ids=true | all-gather | bytes 199680 | tf_op jit(solution)/shard_map/all_gather | solution.py:26
  85.5 0.1 squeeze.203
  85.5 0.1 squeeze.202
  85.6 0.1 squeeze.199
  85.7 0.1 squeeze.200
  85.8 0.1 div.31
  86.0 0.1 mul.551
  86.1 0.1 mul.548
  86.2 0.6 copy.29
  86.9 21.7 %all-to-all-start = ((bf16[2,16,512]{2,0,1:T(2,128)(2,1)}), bf16[2,16,512]{2,0,1:T(2,128)(2,1)S(1)}, u32[]{:S(2)}, u32[]{:S(2)}) async-start(bf16[2,16,512]{2,0,1:T(2,128)(2,1)} %copy.29), calls=%async_computation | async-start | bytes 65536 | tf_op jit(solution)/shard_map/all_to_all | solution.py:140
  108.6 0.7 convert_bitcast_fusion
  109.3 23.7 %all-to-all-done = bf16[2,16,512]{2,0,1:T(2,128)(2,1)S(1)} async-done(((bf16[2,16,512]{2,0,1:T(2,128)(2,1)}), bf16[2,16,512]{2,0,1:T(2,128)(2,1)S(1)}, u32[]{:S(2)}, u32[]{:S(2)}) %all-to-all-start) | async-done | bytes 32800 | tf_op jit(solution)/shard_map/all_to_all | solution.py:140
  133.0 0.0 copy-done
  133.0 0.1 fusion.10
  133.1 0.6 copy.31
  133.8 3.5 %all-to-all-start.1 = ((f32[16,2,128]{2,1,0:T(2,128)}), f32[16,2,128]{2,1,0:T(2,128)S(1)}, u32[]{:S(2)}, u32[]{:S(2)}) async-start(f32[16,2,128]{2,1,0:T(2,128)} %copy.31), calls=%async_computation.1 | async-start | bytes 32768 | tf_op jit(solution)/shard_map/all_to_all | solution.py:52
  137.3 0.7 fusion.55
  138.0 23.6 %all-to-all-done.1 = f32[16,2,128]{2,1,0:T(2,128)S(1)} async-done(((f32[16,2,128]{2,1,0:T(2,128)}), f32[16,2,128]{2,1,0:T(2,128)S(1)}, u32[]{:S(2)}, u32[]{:S(2)}) %all-to-all-start.1) | async-done | bytes 16416 | tf_op jit(solution)/shard_map/all_to_all | solution.py:52
  161.6 0.5 reduce_sum.19
  162.2 0.0 all-gather.8.cloned.1.call-done
  162.2 9.5 %fusion.117 = f32[768,128]{0,1:T(8,128)S(1)} fusion(bf16[768,8192]{1,0:T(8,128)(2,1)} %param.8, bf16[8192,128]{1,0:T(8,128)(2,1)} %all-gather.8.cloned.1.call-done), kind=kOutput, calls=%fused_computation.210 | convolution fusion | flops 1610612736 | bytes 15073280 | tf_op jit(solution)/shard_map/dot_general | solution.py:102
  171.6 0.8 fusion.7
  172.4 0.1 fusion.1
  172.5 0.8 copy.32
  (22 shorter events, 0.3 us)
Async XLA Ops:
  7.2 125.8 %copy-start = (bf16[512,128]{1,0:T(8,128)(2,1)S(1)}, bf16[512,128]{1,0:T(8,128)(2,1)}, u32[]{:S(2)}) copy-start(bf16[512,128]{1,0:T(8,128)(2,1)} %param.15) | copy-start | bytes 393220
  7.2 155.0 %all-gather.8.cloned.1.call-start = ((), (), s32[]{:S(2)}) async-start(), calls=%async_computation.2 | async-start | bytes 2129920 | tf_op jit(solution)/shard_map/all_gather | solution.py:104
  86.9 46.1 %all-to-all-start = ((bf16[2,16,512]{2,0,1:T(2,128)(2,1)}), bf16[2,16,512]{2,0,1:T(2,128)(2,1)S(1)}, u32[]{:S(2)}, u32[]{:S(2)}) async-start(bf16[2,16,512]{2,0,1:T(2,128)(2,1)} %copy.29), calls=%async_computation | async-start | bytes 65536 | tf_op jit(solution)/shard_map/all_to_all | solution.py:140
  133.8 27.9 %all-to-all-start.1 = ((f32[16,2,128]{2,1,0:T(2,128)}), f32[16,2,128]{2,1,0:T(2,128)S(1)}, u32[]{:S(2)}, u32[]{:S(2)}) async-start(f32[16,2,128]{2,1,0:T(2,128)} %copy.31), calls=%async_computation.1 | async-start | bytes 32768 | tf_op jit(solution)/shard_map/all_to_all | solution.py:52
Sparse Core Ops, SparseCore 0:
  10.7 137.7 all-gather.7
where the time goes:
time: 181 us; the launch traced here: 180 us
  blocking collectives  72.4 us (40%)
  waiting for transfers between devices  48 us (27%)
  starting transfers between devices  25.2 us (14%)
  between operations  14.3 us (8%)
  matrix products  11.1 us (6%)
  local copies, waits for them, and re-layouts  4.77 us (3%)
  other arithmetic  4.46 us (2%)
    all_gather x3, blocking collectives, all_in_one(): both, at, found = (lax.all_gather(jnp.concatenate(lines), axis), 0, {})  72.4 us
    all_to_all x1, waiting for transfers between devices, shards(): lax.all_to_all(attention, 'gy', split_axis=1, concat_axis=0, tiled=True)  23.7 us
    all_to_all x1, waiting for transfers between devices, sum_at_owner(): lax.all_to_all(cut_along(shard, dim, devices), axis, 0, 0, tiled=True)  23.6 us
    all_to_all x1, starting transfers between devices, shards(): lax.all_to_all(attention, 'gy', split_axis=1, concat_axis=0, tiled=True)  21.7 us
    dot_general x1, matrix products, shards(): jnp.dot(selected, lax.all_gather(key_value_weight, GX, axis=0, tiled=True...  9.46 us
  transfers between devices with their start and end apart: 3, of which 2 were waited for; matrix products, arithmetic and copies ran while one was open for 5% of the time, Pallas kernels for 0%

commit v1 on v0

v1 whole, which is shorter than its diff:
```python
import jax
import jax.numpy as jnp
from jax import lax
from jax.experimental import pallas as pl
from jax.experimental.pallas import tpu as pltpu
from jax.sharding import PartitionSpec as P

QUERY_HEADS = 64
KEY_VALUE_HEADS = 8
HEAD_SIZE = 128
SLOT = 128
NZ, NX, NC, NY, NK = 8, 4, 2, 4, 4
MESH = pl.DeviceIdType.MESH

rope_base = 500000.0
masked_score = -1e30


def device(z, x, c, y, k):
    return ((z * NX + x) * NC + c, y * NK + k)


def merge(nums, metas):
    metas = [m.astype(jnp.float32) for m in metas]
    peaks = [m[:, 0:1] + m[:, 16:17] + m[:, 32:33] for m in metas]
    totals = [m[:, 48:49] + m[:, 64:65] for m in metas]
    top = peaks[0]
    for p in peaks[1:]:
        top = jnp.maximum(top, p)
    num, den = None, None
    for b, p, t in zip(nums, peaks, totals):
        f = jnp.exp(p - top)
        num = b * f if num is None else num + b * f
        den = t * f if den is None else den + t * f
    return top, den, num


def split(v, terms):
    out = []
    for _ in range(terms):
        part = v.astype(jnp.bfloat16)
        out.append(part)
        v = v - part.astype(jnp.float32)
    return out


def meta_of(top, den):
    lane = lax.broadcasted_iota(jnp.int32, (16, 128), 1)
    wide = [t.astype(jnp.float32) for t in split(top, 3) + split(den, 2)]
    meta = jnp.broadcast_to(wide[4], (16, 128))
    for i in (3, 2, 1, 0):
        meta = jnp.where(lane < 16 * (i + 1), wide[i], meta)
    return meta.astype(jnp.bfloat16)


def kernel(
    lens, tok, kvw, q, cache, w,
    proj, dec,
    tokv, kvb, qv, cachev, wall, sbuf, rbuf1, sbuf2, rbuf2, ag, obuf, rob,
    lsem, s1s, s1r, s2s, s2r, as_, ar, bs, br, w1s, w1r, w2s, w2r, zs, zr, xs, xr, cs, cr, os_, or_,
):
    gx = lax.axis_index("gx")
    gy = lax.axis_index("gy")
    z, x, c = gx // 8, (gx // 2) % 4, gx % 2
    y, k = gy // 4, gy % 4
    xc = gx % 8
    up, down = (k + 1) % 4, (k + 3) % 4
    zpeer = [(z + d) % 8 for d in range(1, 8)]
    xcpeer = [(xc + d) % 8 for d in range(1, 8)]
    ypeer = [(y + d) % 4 for d in range(1, 4)]
    xpeer = [(x + d) % 4 for d in range(1, 4)]

    barrier = pltpu.get_barrier_semaphore()
    peers = [device(t, x, c, y, k) for t in zpeer]
    peers += [device(z, t // 2, t % 2, y, k) for t in xcpeer]
    peers += [device(z, x, c, t, k) for t in ypeer]
    peers += [device(z, x, c, y, t) for t in (up, down)]
    for p in peers:
        pl.semaphore_signal(barrier, inc=1, device_id=p, device_id_type=MESH)

    load_q = pltpu.make_async_copy(q, qv, lsem.at[0])
    load_c = pltpu.make_async_copy(cache, cachev, lsem.at[1])
    load_w = pltpu.make_async_copy(w, wall.at[y, pl.ds(0, 512)], lsem.at[2])
    load_k = pltpu.make_async_copy(kvw, kvb.at[z, x, c], lsem.at[3])
    load_t = pltpu.make_async_copy(tok, tokv, lsem.at[4])
    for l in (load_q, load_c, load_w, load_k, load_t):
        l.start()

    load_q.wait()
    load_c.wait()
    q32 = qv[...].astype(jnp.float32)
    row = lax.broadcasted_iota(jnp.int32, (16, 128), 0)
    lane = lax.broadcasted_iota(jnp.int32, (16, 128), 1)
    length = jnp.where(row < 8, lens[0], lens[1])
    valid = gx * 128 + lane < length
    for g in range(8):
        rows = [
            q32[b : b + 1, h * 128 : (h + 1) * 128]
            for b in range(2)
            for h in range(g * 8, g * 8 + 8)
        ]
        q16 = jnp.concatenate(rows, axis=0).astype(jnp.bfloat16)
        cols = slice(g * 128, (g + 1) * 128)
        dn = (((1,), (1,)), ((), ()))
        both = [
            lax.dot_general(q16, cachev[0, b, :, cols], dn, preferred_element_type=jnp.float32)
            for b in range(2)
        ]
        score = jnp.where(row < 8, both[0], both[1]) * HEAD_SIZE ** (-0.5)
        peak = jnp.max(jnp.where(valid, score, masked_score), axis=1, keepdims=True)
        weight = jnp.where(valid, jnp.exp(score - peak), 0.0)
        total = jnp.sum(weight, axis=1, keepdims=True)
        w16 = weight.astype(jnp.bfloat16)
        both = [
            jnp.dot(w16, cachev[1, b, :, cols], preferred_element_type=jnp.float32)
            for b in range(2)
        ]
        sbuf[g, :, :128] = jnp.where(row < 8, both[0], both[1]).astype(jnp.bfloat16)
        sbuf[g, :, 128:] = meta_of(peak, total)

    pl.semaphore_wait(barrier, len(peers))

    def remote(src, dst, ss, rs, dev):
        return pltpu.make_async_remote_copy(
            src_ref=src, dst_ref=dst, send_sem=ss, recv_sem=rs, device_id=dev, device_id_type=MESH
        )

    sends = []

    def go(cp):
        cp.start()
        sends.append(cp)

    for t in zpeer:
        go(remote(sbuf.at[t], rbuf1.at[z], s1s.at[t], s1r.at[z], device(t, x, c, y, k)))
    load_w.wait()
    go(remote(wall.at[y, pl.ds(0, 256)], wall.at[y, pl.ds(512, 256)], w1s.at[0], w1r.at[0], device(z, x, c, y, up)))
    go(remote(wall.at[y, pl.ds(256, 256)], wall.at[y, pl.ds(768, 256)], w1s.at[1], w1r.at[1], device(z, x, c, y, down)))
    for t in ypeer:
        own = wall.at[y, pl.ds(0, 512)]
        go(remote(own, own, w2s.at[0, t], w2r.at[0, y], device(z, x, c, t, k)))
    load_k.wait()
    for t in zpeer:
        own = kvb.at[z, x, c]
        go(remote(own, own, zs.at[t], zr.at[z], device(t, x, c, y, k)))

    here = device(z, x, c, y, k)
    for t in zpeer:
        remote(sbuf.at[t], rbuf1.at[t], s1s.at[t], s1r.at[t], here).wait_recv()
    blocks = [sbuf[z]] + [rbuf1[t] for t in zpeer]
    top, den, num = merge([b[:, :128].astype(jnp.float32) for b in blocks], [b[:, 128:] for b in blocks])
    high, low = split(num, 2)
    sbuf2[:, :128] = high
    sbuf2[:, 128:256] = low
    sbuf2[:, 256:] = meta_of(top, den)
    for t in xcpeer:
        go(remote(sbuf2, rbuf2.at[xc], s2s.at[t], s2r.at[xc], device(z, t // 2, t % 2, y, k)))
    for t in xcpeer:
        remote(sbuf2, rbuf2.at[t], s2s.at[t], s2r.at[t], here).wait_recv()
    blocks = [sbuf2[...]] + [rbuf2[t] for t in xcpeer]
    nums = [b[:, :128].astype(jnp.float32) + b[:, 128:256].astype(jnp.float32) for b in blocks]
    top, den, num = merge(nums, [b[:, 256:] for b in blocks])
    ag[0, z] = (num / den).astype(jnp.bfloat16)

    go(remote(ag.at[0, z], ag.at[1, z], as_.at[0], ar.at[0], device(z, x, c, y, up)))
    go(remote(ag.at[0, z], ag.at[2, z], as_.at[1], ar.at[1], device(z, x, c, y, down)))
    for t in zpeer:
        go(remote(ag.at[0, z], ag.at[0, z], bs.at[0, t], br.at[0, z], device(t, x, c, y, k)))

    for t in zpeer:
        remote(kvb.at[t, x, c], kvb.at[t, x, c], zs.at[t], zr.at[t], here).wait_recv()
    for t in xpeer:
        own = kvb.at[:, x, c]
        go(remote(own, own, xs.at[t], xr.at[x], device(z, t, c, y, k)))

    for s in (1, 2):
        remote(ag.at[0, z], ag.at[s, z], as_.at[s - 1], ar.at[s - 1], here).wait_recv()
        for t in zpeer:
            go(remote(ag.at[s, z], ag.at[s, z], bs.at[s, t], br.at[s, z], device(t, x, c, y, k)))

    for i, lo in ((0, 512), (1, 768)):
        part = wall.at[y, pl.ds(lo, 256)]
        remote(part, part, w1s.at[i], w1r.at[i], here).wait_recv()
    for t in ypeer:
        part = wall.at[y, pl.ds(512, 512)]
        go(remote(part, part, w2s.at[1, t], w2r.at[1, y], device(z, x, c, t, k)))

    for t in xpeer:
        part = kvb.at[:, t, c]
        remote(part, part, xs.at[t], xr.at[t], here).wait_recv()
    own = kvb.at[:, :, c]
    go(remote(own, own, cs, cr, device(z, x, 1 - c, y, k)))

    for s in range(3):
        for t in zpeer:
            remote(ag.at[s, t], ag.at[s, t], bs.at[s, t], br.at[s, t], here).wait_recv()
    for i in range(2):
        for t in ypeer:
            part = wall.at[t, pl.ds(512 * i, 512)]
            remote(part, part, w2s.at[i, t], w2r.at[i, t], here).wait_recv()

    row16 = lax.broadcasted_iota(jnp.int32, (16, 128), 0) % 8
    zero = jnp.zeros((16, 128), jnp.bfloat16)
    acc = jnp.zeros((48, 128), jnp.float32)
    for yy in range(4):
        cols = []
        for d, r in ((0, 0), (0, 1), (0, 2), (0, 3), (3, 0), (3, 1), (1, 2), (1, 3)):
            zh = (k + d) % 4
            keep = row16 == (zh % 2) * 4 + r
            use = {(0, 0): (0, 1), (0, 1): (0, 1), (0, 2): (0, 2), (0, 3): (0, 2)}.get((d, r))
            use = use or ((0, 2) if d == 3 else (0, 1))
            col = []
            for s in range(3):
                if s in use:
                    tile = ag[s, 2 * yy + zh // 2].astype(jnp.float32)
                    col.append(jnp.where(keep, tile, 0.0).astype(jnp.bfloat16))
                else:
                    col.append(zero)
            cols.append(jnp.concatenate(col, axis=0))
        lhs = jnp.concatenate(cols, axis=1)
        acc += jnp.dot(lhs, wall[yy], preferred_element_type=jnp.float32)
    sums = [jnp.sum(acc[8 * i : 8 * i + 8], axis=0, keepdims=True) for i in range(6)]
    obuf[...] = jnp.concatenate(sums + [jnp.zeros((2, 128), jnp.float32)], axis=0)
    go(remote(obuf, rob.at[0], os_.at[0], or_.at[0], device(z, x, c, y, down)))
    go(remote(obuf, rob.at[1], os_.at[1], or_.at[1], device(z, x, c, y, up)))

    other = kvb.at[:, :, 1 - c]
    remote(other, other, cs, cr, here).wait_recv()
    load_t.wait()
    proj[...] = jnp.zeros_like(proj)

    @pl.loop(0, 8)
    def _(i):
        lhs = tokv[:, pl.ds(pl.multiple_of(i * 1024, 1024), 1024)]
        rhs = kvb[i].reshape(1024, 128)
        proj[...] += jnp.dot(lhs, rhs, preferred_element_type=jnp.float32)

    for i in range(2):
        remote(obuf, rob.at[i], os_.at[i], or_.at[i], here).wait_recv()
    dec[0:2] = obuf[0:2] + rob[0, 2:4] + rob[1, 4:6]
    for s in sends:
        s.wait_send()


def rotate_and_mask(projected, is_key, prefix_lengths, start_offsets):
    tok_rows = projected.shape[0]
    slot_index = jnp.arange(SLOT, dtype=jnp.int32)
    positions = (start_offsets[:, None] + slot_index[None, :]).reshape(tok_rows)
    live_rows = (slot_index[None, :] < prefix_lengths[:, None]).reshape(tok_rows)
    half_width = HEAD_SIZE // 2
    freq_index = jnp.arange(half_width, dtype=jnp.float32)
    inverse = rope_base ** (-2.0 * freq_index / HEAD_SIZE)
    angles = positions.astype(jnp.float32)[:, None] * inverse[None, :]
    cosine = jnp.cos(angles)
    sine = jnp.sin(angles)
    first_half = projected[:, :half_width]
    second_half = projected[:, half_width:]
    rotated = jnp.concatenate(
        [first_half * cosine - second_half * sine, second_half * cosine + first_half * sine], axis=1
    )
    kept = jnp.where(live_rows[:, None], jnp.where(is_key, rotated, projected), 0.0)
    return kept.astype(jnp.bfloat16)


def shards(tok, kvw, prefix_lengths, start_offsets, q, cache, lens, w):
    bf, f32 = jnp.bfloat16, jnp.float32
    vm = pltpu.VMEM
    dma = pltpu.SemaphoreType.DMA
    any_ = pl.BlockSpec(memory_space=pl.ANY)
    vmem = pl.BlockSpec(memory_space=pltpu.VMEM)
    proj, dec = pl.pallas_call(
        kernel,
        out_shape=(jax.ShapeDtypeStruct((tok.shape[0], 128), f32), jax.ShapeDtypeStruct((2, 128), f32)),
        in_specs=[pl.BlockSpec(memory_space=pltpu.SMEM)] + [any_] * 5,
        out_specs=(vmem, vmem),
        scratch_shapes=[
            vm(tok.shape, bf), vm((8, 4, 2, 128, 128), bf), vm(q.shape, bf), vm(cache.shape, bf),
            vm((4, 1024, 128), bf), vm((8, 16, 256), bf), vm((8, 16, 256), bf), vm((16, 384), bf),
            vm((8, 16, 384), bf), vm((3, 8, 16, 128), bf), vm((8, 128), f32), vm((2, 8, 128), f32),
            dma((5,)), dma((8,)), dma((8,)), dma((8,)), dma((8,)), dma((2,)), dma((2,)),
            dma((3, 8)), dma((3, 8)), dma((2,)), dma((2,)), dma((2, 4)), dma((2, 4)),
            dma((8,)), dma((8,)), dma((4,)), dma((4,)), dma, dma, dma((2,)), dma((2,)),
        ],
        compiler_params=pltpu.CompilerParams(
            collective_id=0, has_side_effects=True, vmem_limit_bytes=40 * 1024 * 1024
        ),
    )(lens, tok, kvw, q, cache, w)
    is_key = lax.axis_index("gy") < KEY_VALUE_HEADS
    return rotate_and_mask(proj, is_key, prefix_lengths, start_offsets), dec.astype(jnp.bfloat16)


def solution(mesh):
    return jax.shard_map(
        shards,
        mesh=mesh,
        in_specs=(
            P("gx", None), P("gx", "gy"), P("gx"), P("gx"), P("gy", None),
            P(None, "gy", "gx", None), P("gy"), P("gy", "gx"),
        ),
        out_specs=(P("gx", "gy"), P("gy", "gx")),
        check_vma=False,
    )
```

time: 181 us -> 87.2 us (0.48)
  the two profiles are of different devices: /device:TPU:2 before, /device:TPU:120 now
where the time goes in v1:
time: 87.2 us; the launch traced here: 86.8 us
  Pallas kernels  72.6 us (83%)
  local copies, waits for them, and re-layouts  8.87 us (10%)
  other arithmetic  4.68 us (5%)
    pallas_call x1, Pallas kernels, shards(): pl.pallas_call(kernel, out_shape=(jax.ShapeDtypeStruct((tok.shape[0], 128...  72.6 us
    unnamed x12, local copies, waits for them, and re-layouts  8.87 us
    sub x1, other arithmetic, rotate_and_mask(): first_half * cosine - second_half * sine  1.8 us

profile of v1, /device:TPU:120, one launch (start us, length us, event | category | flops | bytes accessed | tf_op | source)
XLA Modules:
  0.0 86.8 jit_solution(1534133412955530621)
XLA Ops:
  0.6 0.7 fusion.8
  1.4 0.7 convert_bitcast_fusion
  2.1 0.0 copy-start
  2.1 4.6 %copy-done = bf16[768,8192]{1,0:T(8,128)(2,1)S(1)} copy-done((bf16[768,8192]{1,0:T(8,128)(2,1)S(1)}, bf16[768,8192]{1,0:T(8,128)(2,1)}, u32[]{:S(2)}) %copy-start) | copy-done | bytes 12582936
  6.7 0.0 copy-start.1
  6.7 1.2 %copy-done.1 = bf16[2,2,128,1024]{3,2,1,0:T(8,128)(2,1)S(1)} copy-done((bf16[2,2,128,1024]{3,2,1,0:T(8,128)(2,1)S(1)}, bf16[2,2,128,1024]{3,2,1,0:T(8,128)(2,1)}, u32[]{:S(2)}) %copy-start.1) | copy-done | bytes 1048600
  7.9 0.0 copy-start.2
  7.9 0.9 %copy-done.2 = bf16[512,128]{1,0:T(8,128)(2,1)S(1)} copy-done((bf16[512,128]{1,0:T(8,128)(2,1)S(1)}, bf16[512,128]{1,0:T(8,128)(2,1)}, u32[]{:S(2)}) %copy-start.2) | copy-done | bytes 131096
  8.8 0.0 copy-start.3
  8.8 0.8 copy-done.3
  9.6 0.0 copy-start.4
  9.6 0.8 copy-done.4
  10.3 0.0 copy-start.5
  10.3 0.7 copy-done.5
  11.0 72.6 %shard_map.95 = (f32[768,128]{1,0:T(8,128)S(1)}, f32[2,128]{1,0:T(2,128)S(1)}) custom-call(s32[2]{0:T(128)S(1)} %copy-done.5, bf16[768,8192]{1,0:T(8,128)(2,1)S(1)} %copy-done, bf16[128,128]{1,0:T(8,128)(2,1)S(1)} %copy-done.3, bf16[2,8192]{1,0:T(2,128)(2,1)S(1)} %copy-done.4, bf16[2,2,128,1024]{3,2,1,0:T(8,128)(2,1)S(1)} %copy-done.1, ...), custom_call_target="tpu_custom_call" | custom-call | tf_op jit(solution)/shard_map/pallas_call | solution.py:271
  83.6 0.5 convert_element_type.19
  84.1 1.8 %fusion.4 = (bf16[768,64]{1,0:T(8,128)(2,1)S(1)}, bf16[768,64]{1,0:T(8,128)(2,1)S(1)}) fusion(f32[768,128]{1,0:T(8,128)S(1)} %get-tuple-element.4, f32[64]{0:T(128)S(1)} %multiply_power_fusion, f32[768]{0:T(1024)S(1)} %convert_bitcast_fusion), kind=kLoop, calls=%fused_computation.6 | loop fusion | flops 442368 | bytes 593152 | tf_op jit(solution)/shard_map/sub | solution.py:259
  85.9 0.9 %fusion.7 = bf16[768,128]{1,0:T(8,128)(2,1)} fusion(f32[768,128]{1,0:T(8,128)S(1)} %get-tuple-element.4, bf16[768,64]{1,0:T(8,128)(2,1)S(1)} %get-tuple-element.7, bf16[768,64]{1,0:T(8,128)(2,1)S(1)} %get-tuple-element.6, pred[768]{0:T(1024)(128)(4,1)S(1)} %fusion.8, pred[]{:T(512)S(6)} %lt.29), kind=kLoop, calls=%fused_computation.10 | loop fusion | flops 589824 | bytes 787201 | tf_op jit(solution)/shard_map/convert_element_type | solution.py:262
  (1 shorter events, 0.0 us)
Async XLA Ops:
  2.1 4.6 %copy-start = (bf16[768,8192]{1,0:T(8,128)(2,1)S(1)}, bf16[768,8192]{1,0:T(8,128)(2,1)}, u32[]{:S(2)}) copy-start(bf16[768,8192]{1,0:T(8,128)(2,1)} %tok.1) | copy-start | bytes 37748740
  6.7 1.2 %copy-start.1 = (bf16[2,2,128,1024]{3,2,1,0:T(8,128)(2,1)S(1)}, bf16[2,2,128,1024]{3,2,1,0:T(8,128)(2,1)}, u32[]{:S(2)}) copy-start(bf16[2,2,128,1024]{3,2,1,0:T(8,128)(2,1)} %cache.1) | copy-start | bytes 3145732
  7.9 0.9 %copy-start.2 = (bf16[512,128]{1,0:T(8,128)(2,1)S(1)}, bf16[512,128]{1,0:T(8,128)(2,1)}, u32[]{:S(2)}) copy-start(bf16[512,128]{1,0:T(8,128)(2,1)} %w.1) | copy-start | bytes 393220
  8.8 0.8 copy-start.3
  9.6 0.8 copy-start.4
  10.3 0.7 copy-start.5

commit v2 on v1

--- a/solution.py
+++ b/solution.py
@@ -1,5 +1,6 @@
 import jax
 import jax.numpy as jnp
+import numpy as np
 from jax import lax
 from jax.experimental import pallas as pl
 from jax.experimental.pallas import tpu as pltpu
@@ -53,11 +54,28 @@
     return meta.astype(jnp.bfloat16)
 
 
+def turn(angle):
+    n = jnp.floor(angle * (2.0 / np.pi) + 0.5)
+    r = angle - n * 1.5703125
+    r = r - n * 4.837512969970703125e-4
+    r = r - n * 7.54978995489188216e-8
+    z = r * r
+    s = ((-1.9515295891e-4 * z + 8.3321608736e-3) * z - 1.6666654611e-1) * z * r + r
+    c = ((2.443315711809948e-5 * z - 1.388731625493765e-3) * z + 4.166664568298827e-2) * z * z - 0.5 * z + 1.0
+    quarter = n - 4.0 * jnp.floor(n * 0.25)
+    odd = (quarter == 1.0) | (quarter == 3.0)
+    cosine = jnp.where(odd, s, c)
+    sine = jnp.where(odd, c, s)
+    cosine = jnp.where((quarter == 1.0) | (quarter == 2.0), -cosine, cosine)
+    sine = jnp.where(quarter >= 2.0, -sine, sine)
+    return cosine, sine
+
+
 def kernel(
-    lens, tok, kvw, q, cache, w,
-    proj, dec,
-    tokv, kvb, qv, cachev, wall, sbuf, rbuf1, sbuf2, rbuf2, ag, obuf, rob,
-    lsem, s1s, s1r, s2s, s2r, as_, ar, bs, br, w1s, w1r, w2s, w2r, zs, zr, xs, xr, cs, cr, os_, or_,
+    lens, plen, start, inv, tok, kvw, q, cache, w,
+    kv_out, dec,
+    proj, cos_t, sin_t, tokv, kvb, qv, cachev, wall, sbuf, rbuf1, sbuf2, rbuf2, ag, obuf, rob,
+    lsem, s1s, s1r, s2s, s2r, as_, ar, bs, br, w1s, w1r, w2s, w2r, zs, zr, xs, xr, cs, cr, os_, or_, far,
 ):
     gx = lax.axis_index("gx")
     gy = lax.axis_index("gy")
@@ -74,9 +92,18 @@
     peers = [device(t, x, c, y, k) for t in zpeer]
     peers += [device(z, t // 2, t % 2, y, k) for t in xcpeer]
     peers += [device(z, x, c, t, k) for t in ypeer]
-    peers += [device(z, x, c, y, t) for t in (up, down)]
     for p in peers:
         pl.semaphore_signal(barrier, inc=1, device_id=p, device_id_type=MESH)
+    first, last = z == 0, z == NZ - 1
+    above, below = device(0, x, c, y, up), device(NZ - 1, x, c, y, down)
+
+    @pl.when(last)
+    def _():
+        pl.semaphore_signal(barrier, inc=1, device_id=above, device_id_type=MESH)
+
+    @pl.when(first)
+    def _():
+        pl.semaphore_signal(barrier, inc=1, device_id=below, device_id_type=MESH)
 
     load_q = pltpu.make_async_copy(q, qv, lsem.at[0])
     load_c = pltpu.make_async_copy(cache, cachev, lsem.at[1])
@@ -118,7 +145,23 @@
         sbuf[g, :, :128] = jnp.where(row < 8, both[0], both[1]).astype(jnp.bfloat16)
         sbuf[g, :, 128:] = meta_of(peak, total)
 
-    pl.semaphore_wait(barrier, len(peers))
+    sign = jnp.where(lax.broadcasted_iota(jnp.int32, (SLOT, 128), 1) < 64, -1.0, 1.0)
+    slot = lax.broadcasted_iota(jnp.int32, (SLOT, 128), 0)
+    for i in range(plen.shape[0]):
+        angle = (start[i] + slot).astype(jnp.float32) * inv[...]
+        cosine, sine = turn(angle)
+        cos_t[i * SLOT : (i + 1) * SLOT] = cosine
+        sin_t[i * SLOT : (i + 1) * SLOT] = sine * sign
+
+    pl.semaphore_wait(barrier, len(peers) + (z + 6) // 13 + (NZ - z) // NZ)
+
+    @pl.when(last)
+    def _():
+        pl.semaphore_signal(far.at[0], inc=1, device_id=above, device_id_type=MESH)
+
+    @pl.when(first)
+    def _():
+        pl.semaphore_signal(far.at[1], inc=1, device_id=below, device_id_type=MESH)
 
     def remote(src, dst, ss, rs, dev):
         return pltpu.make_async_remote_copy(
@@ -133,20 +176,35 @@
 
     for t in zpeer:
         go(remote(sbuf.at[t], rbuf1.at[z], s1s.at[t], s1r.at[z], device(t, x, c, y, k)))
+    load_k.wait()
+    for t in zpeer:
+        own = kvb.at[z, x, c]
+        go(remote(own, own, zs.at[t], zr.at[z], device(t, x, c, y, k)))
+
     load_w.wait()
-    go(remote(wall.at[y, pl.ds(0, 256)], wall.at[y, pl.ds(512, 256)], w1s.at[0], w1r.at[0], device(z, x, c, y, up)))
-    go(remote(wall.at[y, pl.ds(256, 256)], wall.at[y, pl.ds(768, 256)], w1s.at[1], w1r.at[1], device(z, x, c, y, down)))
     for t in ypeer:
         own = wall.at[y, pl.ds(0, 512)]
         go(remote(own, own, w2s.at[0, t], w2r.at[0, y], device(z, x, c, t, k)))
-    load_k.wait()
-    for t in zpeer:
-        own = kvb.at[z, x, c]
-        go(remote(own, own, zs.at[t], zr.at[z], device(t, x, c, y, k)))
+
+    for flag, end in ((0, first), (1, last)):
+
+        @pl.when(end)
+        def _():
+            pl.semaphore_wait(far.at[flag], 1)
+            for t in zpeer:
+                pl.semaphore_signal(far.at[flag], inc=1, device_id=device(t, x, c, y, k), device_id_type=MESH)
 
     here = device(z, x, c, y, k)
     for t in zpeer:
         remote(sbuf.at[t], rbuf1.at[t], s1s.at[t], s1r.at[t], here).wait_recv()
+    for flag, end in ((0, first), (1, last)):
+
+        @pl.when(jnp.logical_not(end))
+        def _():
+            pl.semaphore_wait(far.at[flag], 1)
+
+    go(remote(wall.at[y, pl.ds(0, 256)], wall.at[y, pl.ds(512, 256)], w1s.at[0], w1r.at[0], device(z, x, c, y, up)))
+    go(remote(wall.at[y, pl.ds(256, 256)], wall.at[y, pl.ds(768, 256)], w1s.at[1], w1r.at[1], device(z, x, c, y, down)))
     blocks = [sbuf[z]] + [rbuf1[t] for t in zpeer]
     top, den, num = merge([b[:, :128].astype(jnp.float32) for b in blocks], [b[:, 128:] for b in blocks])
     high, low = split(num, 2)
@@ -173,17 +231,17 @@
         own = kvb.at[:, x, c]
         go(remote(own, own, xs.at[t], xr.at[x], device(z, t, c, y, k)))
 
-    for s in (1, 2):
-        remote(ag.at[0, z], ag.at[s, z], as_.at[s - 1], ar.at[s - 1], here).wait_recv()
-        for t in zpeer:
-            go(remote(ag.at[s, z], ag.at[s, z], bs.at[s, t], br.at[s, z], device(t, x, c, y, k)))
-
     for i, lo in ((0, 512), (1, 768)):
         part = wall.at[y, pl.ds(lo, 256)]
         remote(part, part, w1s.at[i], w1r.at[i], here).wait_recv()
     for t in ypeer:
         part = wall.at[y, pl.ds(512, 512)]
         go(remote(part, part, w2s.at[1, t], w2r.at[1, y], device(z, x, c, t, k)))
+
+    for s in (1, 2):
+        remote(ag.at[0, z], ag.at[s, z], as_.at[s - 1], ar.at[s - 1], here).wait_recv()
+        for t in zpeer:
+            go(remote(ag.at[s, z], ag.at[s, z], bs.at[s, t], br.at[s, z], device(t, x, c, y, k)))
 
     for t in xpeer:
         part = kvb.at[:, t, c]
@@ -235,58 +293,49 @@
         rhs = kvb[i].reshape(1024, 128)
         proj[...] += jnp.dot(lhs, rhs, preferred_element_type=jnp.float32)
 
+    is_key = gy < KEY_VALUE_HEADS
+    for i in range(plen.shape[0]):
+        rows = slice(i * SLOT, (i + 1) * SLOT)
+        plain = proj[rows]
+        turned = plain * cos_t[rows] + pltpu.roll(plain, 64, 1) * sin_t[rows]
+        kept = jnp.where(slot < plen[i], jnp.where(is_key, turned, plain), 0.0)
+        kv_out[rows] = kept.astype(jnp.bfloat16)
+
     for i in range(2):
         remote(obuf, rob.at[i], os_.at[i], or_.at[i], here).wait_recv()
-    dec[0:2] = obuf[0:2] + rob[0, 2:4] + rob[1, 4:6]
+    dec[...] = (obuf[0:2] + rob[0, 2:4] + rob[1, 4:6]).astype(jnp.bfloat16)
     for s in sends:
         s.wait_send()
-
-
-def rotate_and_mask(projected, is_key, prefix_lengths, start_offsets):
-    tok_rows = projected.shape[0]
-    slot_index = jnp.arange(SLOT, dtype=jnp.int32)
-    positions = (start_offsets[:, None] + slot_index[None, :]).reshape(tok_rows)
-    live_rows = (slot_index[None, :] < prefix_lengths[:, None]).reshape(tok_rows)
-    half_width = HEAD_SIZE // 2
-    freq_index = jnp.arange(half_width, dtype=jnp.float32)
-    inverse = rope_base ** (-2.0 * freq_index / HEAD_SIZE)
-    angles = positions.astype(jnp.float32)[:, None] * inverse[None, :]
-    cosine = jnp.cos(angles)
-    sine = jnp.sin(angles)
-    first_half = projected[:, :half_width]
-    second_half = projected[:, half_width:]
-    rotated = jnp.concatenate(
-        [first_half * cosine - second_half * sine, second_half * cosine + first_half * sine], axis=1
-    )
-    kept = jnp.where(live_rows[:, None], jnp.where(is_key, rotated, projected), 0.0)
-    return kept.astype(jnp.bfloat16)
 
 
 def shards(tok, kvw, prefix_lengths, start_offsets, q, cache, lens, w):
     bf, f32 = jnp.bfloat16, jnp.float32
     vm = pltpu.VMEM
     dma = pltpu.SemaphoreType.DMA
-    any_ = pl.BlockSpec(memory_space=pl.ANY)
+    hbm = pl.BlockSpec(memory_space=pltpu.HBM)
+    smem = pl.BlockSpec(memory_space=pltpu.SMEM)
     vmem = pl.BlockSpec(memory_space=pltpu.VMEM)
-    proj, dec = pl.pallas_call(
+    inverse = rope_base ** (-2.0 * (np.arange(128) % 64) / HEAD_SIZE)
+    prefix_kv, dec = pl.pallas_call(
         kernel,
-        out_shape=(jax.ShapeDtypeStruct((tok.shape[0], 128), f32), jax.ShapeDtypeStruct((2, 128), f32)),
-        in_specs=[pl.BlockSpec(memory_space=pltpu.SMEM)] + [any_] * 5,
+        out_shape=(jax.ShapeDtypeStruct((tok.shape[0], 128), bf), jax.ShapeDtypeStruct((2, 128), bf)),
+        in_specs=[smem] * 3 + [vmem] + [hbm] * 5,
         out_specs=(vmem, vmem),
         scratch_shapes=[
+            vm((tok.shape[0], 128), f32), vm((tok.shape[0], 128), f32), vm((tok.shape[0], 128), f32),
             vm(tok.shape, bf), vm((8, 4, 2, 128, 128), bf), vm(q.shape, bf), vm(cache.shape, bf),
             vm((4, 1024, 128), bf), vm((8, 16, 256), bf), vm((8, 16, 256), bf), vm((16, 384), bf),
             vm((8, 16, 384), bf), vm((3, 8, 16, 128), bf), vm((8, 128), f32), vm((2, 8, 128), f32),
             dma((5,)), dma((8,)), dma((8,)), dma((8,)), dma((8,)), dma((2,)), dma((2,)),
             dma((3, 8)), dma((3, 8)), dma((2,)), dma((2,)), dma((2, 4)), dma((2, 4)),
             dma((8,)), dma((8,)), dma((4,)), dma((4,)), dma, dma, dma((2,)), dma((2,)),
+            pltpu.SemaphoreType.REGULAR((2,)),
         ],
         compiler_params=pltpu.CompilerParams(
-            collective_id=0, has_side_effects=True, vmem_limit_bytes=40 * 1024 * 1024
+            collective_id=0, has_side_effects=True, vmem_limit_bytes=67043328
         ),
-    )(lens, tok, kvw, q, cache, w)
-    is_key = lax.axis_index("gy") < KEY_VALUE_HEADS
-    return rotate_and_mask(proj, is_key, prefix_lengths, start_offsets), dec.astype(jnp.bfloat16)
+    )(lens, prefix_lengths, start_offsets, np.float32(inverse)[None, :], tok, kvw, q, cache, w)
+    return prefix_kv, dec
 
 
 def solution(mesh):

time: 87.2 us -> 75.4 us (0.86)
  the two profiles are of different devices: /device:TPU:120 before, /device:TPU:66 now
where the time goes in v2:
time: 75.4 us; the launch traced here: 75.2 us
  Pallas kernels  71.9 us (95%)
  local copies, waits for them, and re-layouts  2.75 us (4%)
    pallas_call x1, Pallas kernels, shards(): pl.pallas_call(kernel, out_shape=(jax.ShapeDtypeStruct((tok.shape[0], 128...  71.9 us
    unnamed x2, local copies, waits for them, and re-layouts  2.75 us

profile of v2, /device:TPU:66, one launch (start us, length us, event | category | flops | bytes accessed | tf_op | source)
XLA Modules:
  0.0 75.2 jit_solution(6457626475735530286)
XLA Ops:
  0.6 71.9 %shard_map.104 = (bf16[768,128]{1,0:T(8,128)(2,1)}, bf16[2,128]{1,0:T(2,128)(2,1)}) custom-call(s32[2]{0:T(128)} %lens.1, s32[6]{0:T(128)} %plen.1, s32[6]{0:T(128)} %start.1, f32[1,128]{1,0:T(1,128)} %constant.2.clone.inv, bf16[768,8192]{1,0:T(8,128)(2,1)} %tok.1, bf16[128,128]{1,0:T(8,128)(2,1)} %kvw.1, bf16[2,8192]{1,0:T(2,128)(2,1)} %q.1, ...), custom_call_target="tpu_custom_call" | custom-call | tf_op jit(solution)/shard_map/pallas_call | solution.py:319
  72.5 1.6 %copy.13 = bf16[768,128]{1,0:T(8,128)(2,1)} copy(bf16[768,128]{1,0:T(8,128)(2,1)} %get-tuple-element.4) | data formatting | bytes 393216
  74.1 1.1 %copy.14 = bf16[2,128]{1,0:T(2,128)(2,1)} copy(bf16[2,128]{1,0:T(2,128)(2,1)} %get-tuple-element.5) | data formatting | bytes 1024

commit v3 on v2

--- a/solution.py
+++ b/solution.py
@@ -110,11 +110,12 @@
     load_w = pltpu.make_async_copy(w, wall.at[y, pl.ds(0, 512)], lsem.at[2])
     load_k = pltpu.make_async_copy(kvw, kvb.at[z, x, c], lsem.at[3])
     load_t = pltpu.make_async_copy(tok, tokv, lsem.at[4])
-    for l in (load_q, load_c, load_w, load_k, load_t):
+    for l in (load_q, load_c, load_k, load_w):
         l.start()
 
     load_q.wait()
     load_c.wait()
+    load_t.start()
     q32 = qv[...].astype(jnp.float32)
     row = lax.broadcasted_iota(jnp.int32, (16, 128), 0)
     lane = lax.broadcasted_iota(jnp.int32, (16, 128), 1)
@@ -145,6 +146,61 @@
         sbuf[g, :, :128] = jnp.where(row < 8, both[0], both[1]).astype(jnp.bfloat16)
         sbuf[g, :, 128:] = meta_of(peak, total)
 
+    pl.semaphore_wait(barrier, len(peers) + (z + 6) // 13 + (NZ - z) // NZ)
+
+    @pl.when(last)
+    def _():
+        pl.semaphore_signal(far.at[0], inc=1, device_id=above, device_id_type=MESH)
+
+    @pl.when(first)
+    def _():
+        pl.semaphore_signal(far.at[1], inc=1, device_id=below, device_id_type=MESH)
+
+    def remote(src, dst, ss, rs, dev):
+        return pltpu.make_async_remote_copy(
+            src_ref=src, dst_ref=dst, send_sem=ss, recv_sem=rs, device_id=dev, device_id_type=MESH
+        )
+
+    sends = []
+
+    def go(cp):
+        cp.start()
+        sends.append(cp)
+
+    for t in zpeer:
+        go(remote(sbuf.at[t], rbuf1.at[z], s1s.at[t], s1r.at[z], device(t, x, c, y, k)))
+    load_k.wait()
+    mate = (z + 4) % 8
+    quad = [z // 4 * 4 + (z + d) % 4 for d in range(1, 4)]
+    far_quad = [mate // 4 * 4 + (z + d) % 4 for d in range(1, 4)]
+    own = kvb.at[z, x, c]
+    for t in [mate] + quad:
+        go(remote(own, own, zs.at[t], zr.at[z], device(t, x, c, y, k)))
+    for u in xpeer:
+        own = kvb.at[z, x, c]
+        go(remote(own, own, xs.at[z, u], xr.at[z, x], device(z, u, c, y, k)))
+
+    for flag, end in ((0, first), (1, last)):
+
+        @pl.when(end)
+        def _():
+            pl.semaphore_wait(far.at[flag], 1)
+            for t in zpeer:
+                pl.semaphore_signal(far.at[flag], inc=1, device_id=device(t, x, c, y, k), device_id_type=MESH)
+
+    for flag, end in ((0, first), (1, last)):
+
+        @pl.when(jnp.logical_not(end))
+        def _():
+            pl.semaphore_wait(far.at[flag], 1)
+
+    load_w.wait()
+    go(remote(wall.at[y, pl.ds(0, 256)], wall.at[y, pl.ds(512, 256)], w1s.at[0], w1r.at[0], device(z, x, c, y, up)))
+    go(remote(wall.at[y, pl.ds(256, 256)], wall.at[y, pl.ds(768, 256)], w1s.at[1], w1r.at[1], device(z, x, c, y, down)))
+    for t in ypeer:
+        own = wall.at[y, pl.ds(0, 512)]
+        go(remote(own, own, w2s.at[0, t], w2r.at[0, y], device(z, x, c, t, k)))
+
     sign = jnp.where(lax.broadcasted_iota(jnp.int32, (SLOT, 128), 1) < 64, -1.0, 1.0)
     slot = lax.broadcasted_iota(jnp.int32, (SLOT, 128), 0)
     for i in range(plen.shape[0]):
@@ -153,58 +209,9 @@
         cos_t[i * SLOT : (i + 1) * SLOT] = cosine
         sin_t[i * SLOT : (i + 1) * SLOT] = sine * sign
 
-    pl.semaphore_wait(barrier, len(peers) + (z + 6) // 13 + (NZ - z) // NZ)
-
-    @pl.when(last)
-    def _():
-        pl.semaphore_signal(far.at[0], inc=1, device_id=above, device_id_type=MESH)
-
-    @pl.when(first)
-    def _():
-        pl.semaphore_signal(far.at[1], inc=1, device_id=below, device_id_type=MESH)
-
-    def remote(src, dst, ss, rs, dev):
-        return pltpu.make_async_remote_copy(
-            src_ref=src, dst_ref=dst, send_sem=ss, recv_sem=rs, device_id=dev, device_id_type=MESH
-        )
-
-    sends = []
-
-    def go(cp):
-        cp.start()
-        sends.append(cp)
-
-    for t in zpeer:
-        go(remote(sbuf.at[t], rbuf1.at[z], s1s.at[t], s1r.at[z], device(t, x, c, y, k)))
-    load_k.wait()
-    for t in zpeer:
-        own = kvb.at[z, x, c]
-        go(remote(own, own, zs.at[t], zr.at[z], device(t, x, c, y, k)))
-
-    load_w.wait()
-    for t in ypeer:
-        own = wall.at[y, pl.ds(0, 512)]
-        go(remote(own, own, w2s.at[0, t], w2r.at[0, y], device(z, x, c, t, k)))
-
-    for flag, end in ((0, first), (1, last)):
-
-        @pl.when(end)
-        def _():
-            pl.semaphore_wait(far.at[flag], 1)
-            for t in zpeer:
-                pl.semaphore_signal(far.at[flag], inc=1, device_id=device(t, x, c, y, k), device_id_type=MESH)
-
     here = device(z, x, c, y, k)
     for t in zpeer:
         remote(sbuf.at[t], rbuf1.at[t], s1s.at[t], s1r.at[t], here).wait_recv()
-    for flag, end in ((0, first), (1, last)):
-
-        @pl.when(jnp.logical_not(end))
-        def _():
-            pl.semaphore_wait(far.at[flag], 1)
-
-    go(remote(wall.at[y, pl.ds(0, 256)], wall.at[y, pl.ds(512, 256)], w1s.at[0], w1r.at[0], device(z, x, c, y, up)))
-    go(remote(wall.at[y, pl.ds(256, 256)], wall.at[y, pl.ds(768, 256)], w1s.at[1], w1r.at[1], device(z, x, c, y, down)))
     blocks = [sbuf[z]] + [rbuf1[t] for t in zpeer]
     top, den, num = merge([b[:, :128].astype(jnp.float32) for b in blocks], [b[:, 128:] for b in blocks])
     high, low = split(num, 2)
@@ -213,6 +220,17 @@
     sbuf2[:, 256:] = meta_of(top, den)
     for t in xcpeer:
         go(remote(sbuf2, rbuf2.at[xc], s2s.at[t], s2r.at[xc], device(z, t // 2, t % 2, y, k)))
+    part = kvb.at[mate, x, c]
+    remote(part, part, zs.at[mate], zr.at[mate], here).wait_recv()
+    for t, u in zip(quad, far_quad):
+        go(remote(part, part, zs.at[u], zr.at[mate], device(t, x, c, y, k)))
+    for u in xpeer:
+        go(remote(part, part, xs.at[mate, u], xr.at[mate, x], device(z, u, c, y, k)))
+    for t in quad:
+        part = kvb.at[t, x, c]
+        remote(part, part, zs.at[t], zr.at[t], here).wait_recv()
+        for u in xpeer:
+            go(remote(part, part, xs.at[t, u], xr.at[t, x], device(z, u, c, y, k)))
     for t in xcpeer:
         remote(sbuf2, rbuf2.at[t], s2s.at[t], s2r.at[t], here).wait_recv()
     blocks = [sbuf2[...]] + [rbuf2[t] for t in xcpeer]
@@ -225,85 +243,109 @@
     for t in zpeer:
         go(remote(ag.at[0, z], ag.at[0, z], bs.at[0, t], br.at[0, z], device(t, x, c, y, k)))
 
-    for t in zpeer:
-        remote(kvb.at[t, x, c], kvb.at[t, x, c], zs.at[t], zr.at[t], here).wait_recv()
-    for t in xpeer:
-        own = kvb.at[:, x, c]
-        go(remote(own, own, xs.at[t], xr.at[x], device(z, t, c, y, k)))
-
-    for i, lo in ((0, 512), (1, 768)):
-        part = wall.at[y, pl.ds(lo, 256)]
-        remote(part, part, w1s.at[i], w1r.at[i], here).wait_recv()
-    for t in ypeer:
-        part = wall.at[y, pl.ds(512, 512)]
-        go(remote(part, part, w2s.at[1, t], w2r.at[1, y], device(z, x, c, t, k)))
-
-    for s in (1, 2):
+    for t in far_quad:
+        part = kvb.at[t, x, c]
+        remote(part, part, zs.at[t], zr.at[t], here).wait_recv()
+        for u in xpeer:
+            go(remote(part, part, xs.at[t, u], xr.at[t, x], device(z, u, c, y, k)))
+
+    near = jnp.where((k == 0) | (k == 3), 2, 1)
+    both = (near, 3 - near)
+    for s in both:
+        part = wall.at[y, pl.ds(pl.multiple_of(256 + 256 * s, 256), 256)]
+        remote(part, part, w1s.at[s - 1], w1r.at[s - 1], here).wait_recv()
+        for t in ypeer:
+            go(remote(part, part, w2s.at[s, t], w2r.at[s, y], device(z, x, c, t, k)))
         remote(ag.at[0, z], ag.at[s, z], as_.at[s - 1], ar.at[s - 1], here).wait_recv()
         for t in zpeer:
             go(remote(ag.at[s, z], ag.at[s, z], bs.at[s, t], br.at[s, z], device(t, x, c, y, k)))
 
-    for t in xpeer:
-        part = kvb.at[:, t, c]
-        remote(part, part, xs.at[t], xr.at[t], here).wait_recv()
+    for u in xpeer:
+        for t in range(NZ):
+            part = kvb.at[t, u, c]
+            remote(part, part, xs.at[t, u], xr.at[t, u], here).wait_recv()
     own = kvb.at[:, :, c]
     go(remote(own, own, cs, cr, device(z, x, 1 - c, y, k)))
 
-    for s in range(3):
+    def prefix():
+        other = kvb.at[:, :, 1 - c]
+        remote(other, other, cs, cr, here).wait_recv()
+        load_t.wait()
+        proj[...] = jnp.zeros_like(proj)
+
+        @pl.loop(0, 8)
+        def _(i):
+            lhs = tokv[:, pl.ds(pl.multiple_of(i * 1024, 1024), 1024)]
+            rhs = kvb[i].reshape(1024, 128)
+            proj[...] += jnp.dot(lhs, rhs, preferred_element_type=jnp.float32)
+
+        is_key = gy < KEY_VALUE_HEADS
+        for i in range(plen.shape[0]):
+            rows = slice(i * SLOT, (i + 1) * SLOT)
+            plain = proj[rows]
+            turned = plain * cos_t[rows] + pltpu.roll(plain, 64, 1) * sin_t[rows]
+            kept = jnp.where(slot < plen[i], jnp.where(is_key, turned, plain), 0.0)
+            kv_out[rows] = kept.astype(jnp.bfloat16)
+
+    @pl.when(k == 0)
+    def _():
+        prefix()
+
+    for t in ypeer:
+        part = wall.at[t, pl.ds(0, 512)]
+        remote(part, part, w2s.at[0, t], w2r.at[0, t], here).wait_recv()
+        for s in (1, 2):
+            part = wall.at[t, pl.ds(256 + 256 * s, 256)]
+            remote(part, part, w2s.at[s, t], w2r.at[s, t], here).wait_recv()
+
+    row16 = lax.broadcasted_iota(jnp.int32, (16, 128), 0) % 8
+
+    def tiles(s):
         for t in zpeer:
             remote(ag.at[s, t], ag.at[s, t], bs.at[s, t], br.at[s, t], here).wait_recv()
+
+    def picked(s, yy, zh, r):
+        tile = ag[s, 2 * yy + zh // 2].astype(jnp.float32)
+        return jnp.where(row16 == (zh % 2) * 4 + r, tile, 0.0).astype(jnp.bfloat16)
+
+    def folded(s, acc):
+        pair = [jnp.sum(acc[0:8], axis=0, keepdims=True), jnp.sum(acc[8:16], axis=0, keepdims=True)]
+        obuf[s] = jnp.concatenate(pair + [jnp.zeros((6, 128), jnp.float32)], axis=0)
+
+    def project(s):
+        tiles(s)
+        acc = jnp.zeros((16, 128), jnp.float32)
+        parts = (
+            (k, jnp.where(s == 1, 0, 2), jnp.where(s == 1, 0, 256)),
+            (jnp.where(s == 1, up, down), jnp.where(s == 1, 2, 0), jnp.where(s == 1, 768, 512)),
+        )
+        for yy in range(4):
+            for zh, r, lo in parts:
+                lhs = jnp.concatenate([picked(s, yy, zh, r), picked(s, yy, zh, r + 1)], axis=1)
+                rhs = wall[yy, pl.ds(pl.multiple_of(lo, 256), 256)]
+                acc += jnp.dot(lhs, rhs, preferred_element_type=jnp.float32)
+        folded(s, acc)
+        to = device(z, x, c, y, (k + 5 - 2 * s) % 4)
+        go(remote(obuf.at[s], rob.at[s - 1], os_.at[s - 1], or_.at[s - 1], to))
+
+    project(both[0])
+    tiles(0)
+    acc = jnp.zeros((16, 128), jnp.float32)
+    for yy in range(4):
+        heads = [(k, r) for r in range(4)] + [(down, 0), (down, 1), (up, 2), (up, 3)]
+        lhs = jnp.concatenate([picked(0, yy, zh, r) for zh, r in heads], axis=1)
+        acc += jnp.dot(lhs, wall[yy], preferred_element_type=jnp.float32)
+    folded(0, acc)
+
+    project(both[1])
+
+    @pl.when(k > 0)
+    def _():
+        prefix()
+
     for i in range(2):
-        for t in ypeer:
-            part = wall.at[t, pl.ds(512 * i, 512)]
-            remote(part, part, w2s.at[i, t], w2r.at[i, t], here).wait_recv()
-
-    row16 = lax.broadcasted_iota(jnp.int32, (16, 128), 0) % 8
-    zero = jnp.zeros((16, 128), jnp.bfloat16)
-    acc = jnp.zeros((48, 128), jnp.float32)
-    for yy in range(4):
-        cols = []
-        for d, r in ((0, 0), (0, 1), (0, 2), (0, 3), (3, 0), (3, 1), (1, 2), (1, 3)):
-            zh = (k + d) % 4
-            keep = row16 == (zh % 2) * 4 + r
-            use = {(0, 0): (0, 1), (0, 1): (0, 1), (0, 2): (0, 2), (0, 3): (0, 2)}.get((d, r))
-            use = use or ((0, 2) if d == 3 else (0, 1))
-            col = []
-            for s in range(3):
-                if s in use:
-                    tile = ag[s, 2 * yy + zh // 2].astype(jnp.float32)
-                    col.append(jnp.where(keep, tile, 0.0).astype(jnp.bfloat16))
-                else:
-                    col.append(zero)
-            cols.append(jnp.concatenate(col, axis=0))
-        lhs = jnp.concatenate(cols, axis=1)
-        acc += jnp.dot(lhs, wall[yy], preferred_element_type=jnp.float32)
-    sums = [jnp.sum(acc[8 * i : 8 * i + 8], axis=0, keepdims=True) for i in range(6)]
-    obuf[...] = jnp.concatenate(sums + [jnp.zeros((2, 128), jnp.float32)], axis=0)
-    go(remote(obuf, rob.at[0], os_.at[0], or_.at[0], device(z, x, c, y, down)))
-    go(remote(obuf, rob.at[1], os_.at[1], or_.at[1], device(z, x, c, y, up)))
-
-    other = kvb.at[:, :, 1 - c]
-    remote(other, other, cs, cr, here).wait_recv()
-    load_t.wait()
-    proj[...] = jnp.zeros_like(proj)
-
-    @pl.loop(0, 8)
-    def _(i):
-        lhs = tokv[:, pl.ds(pl.multiple_of(i * 1024, 1024), 1024)]
-        rhs = kvb[i].reshape(1024, 128)
-        proj[...] += jnp.dot(lhs, rhs, preferred_element_type=jnp.float32)
-
-    is_key = gy < KEY_VALUE_HEADS
-    for i in range(plen.shape[0]):
-        rows = slice(i * SLOT, (i + 1) * SLOT)
-        plain = proj[rows]
-        turned = plain * cos_t[rows] + pltpu.roll(plain, 64, 1) * sin_t[rows]
-        kept = jnp.where(slot < plen[i], jnp.where(is_key, turned, plain), 0.0)
-        kv_out[rows] = kept.astype(jnp.bfloat16)
-
-    for i in range(2):
-        remote(obuf, rob.at[i], os_.at[i], or_.at[i], here).wait_recv()
-    dec[...] = (obuf[0:2] + rob[0, 2:4] + rob[1, 4:6]).astype(jnp.bfloat16)
+        remote(obuf.at[i + 1], rob.at[i], os_.at[i], or_.at[i], here).wait_recv()
+    dec[...] = (obuf[0, 0:2] + rob[0, 0:2] + rob[1, 0:2]).astype(jnp.bfloat16)
     for s in sends:
         s.wait_send()
 
@@ -325,10 +367,10 @@
             vm((tok.shape[0], 128), f32), vm((tok.shape[0], 128), f32), vm((tok.shape[0], 128), f32),
             vm(tok.shape, bf), vm((8, 4, 2, 128, 128), bf), vm(q.shape, bf), vm(cache.shape, bf),
             vm((4, 1024, 128), bf), vm((8, 16, 256), bf), vm((8, 16, 256), bf), vm((16, 384), bf),
-            vm((8, 16, 384), bf), vm((3, 8, 16, 128), bf), vm((8, 128), f32), vm((2, 8, 128), f32),
+            vm((8, 16, 384), bf), vm((3, 8, 16, 128), bf), vm((3, 8, 128), f32), vm((2, 8, 128), f32),
             dma((5,)), dma((8,)), dma((8,)), dma((8,)), dma((8,)), dma((2,)), dma((2,)),
-            dma((3, 8)), dma((3, 8)), dma((2,)), dma((2,)), dma((2, 4)), dma((2, 4)),
-            dma((8,)), dma((8,)), dma((4,)), dma((4,)), dma, dma, dma((2,)), dma((2,)),
+            dma((3, 8)), dma((3, 8)), dma((2,)), dma((2,)), dma((3, 4)), dma((3, 4)),
+            dma((8,)), dma((8,)), dma((8, 4)), dma((8, 4)), dma, dma, dma((2,)), dma((2,)),
             pltpu.SemaphoreType.REGULAR((2,)),
         ],
         compiler_params=pltpu.CompilerParams(

time: 75.4 us -> 67.3 us (0.89)
  the two profiles are of different devices: /device:TPU:66 before, /device:TPU:38 now
where the time goes in v3:
time: 67.3 us; the launch traced here: 67.1 us
  Pallas kernels  63.7 us (95%)
  local copies, waits for them, and re-layouts  2.75 us (4%)
    pallas_call x1, Pallas kernels, shards(): pl.pallas_call(kernel, out_shape=(jax.ShapeDtypeStruct((tok.shape[0], 128...  63.7 us
    unnamed x2, local copies, waits for them, and re-layouts  2.75 us

profile of v3, /device:TPU:38, one launch (start us, length us, event | category | flops | bytes accessed | tf_op | source)
XLA Modules:
  0.0 67.1 jit_solution(15406211588398536133)
XLA Ops:
  0.6 63.7 %shard_map.104 = (bf16[768,128]{1,0:T(8,128)(2,1)}, bf16[2,128]{1,0:T(2,128)(2,1)}) custom-call(s32[2]{0:T(128)} %lens.1, s32[6]{0:T(128)} %plen.1, s32[6]{0:T(128)} %start.1, f32[1,128]{1,0:T(1,128)} %constant.2.clone.inv, bf16[768,8192]{1,0:T(8,128)(2,1)} %tok.1, bf16[128,128]{1,0:T(8,128)(2,1)} %kvw.1, bf16[2,8192]{1,0:T(2,128)(2,1)} %q.1, ...), custom_call_target="tpu_custom_call" | custom-call | tf_op jit(solution)/shard_map/pallas_call | solution.py:361
  64.4 1.6 %copy.13 = bf16[768,128]{1,0:T(8,128)(2,1)} copy(bf16[768,128]{1,0:T(8,128)(2,1)} %get-tuple-element.4) | data formatting | bytes 393216
  66.0 1.1 %copy.14 = bf16[2,128]{1,0:T(2,128)(2,1)} copy(bf16[2,128]{1,0:T(2,128)(2,1)} %get-tuple-element.5) | data formatting | bytes 1024
